TPU v7x, 32 devices: a whole 2x2x4 slice. The times are simulated.
32 devices in a mesh: blk: 16 (over z, x, core), grp: 2 (over y).
Axes of the slice: x: 2, y: 2, z: 4, core: 2. Of those that a mesh axis runs over, the one named last changes fastest.
Arguments:
- left_real: bfloat16 [4096, 8192], P('blk'), may hold values from -6 to 6
- left_imag: bfloat16 [4096, 8192], P('blk'), may hold values from -6 to 6
- right_real: bfloat16 [8192, 512], P('blk', 'grp'), may hold values from -0.0625 to 0.0625
- right_imag: bfloat16 [8192, 512], P('blk', 'grp'), may hold values from -0.0625 to 0.0625
- row_scale: float32 [4096], P('blk'), may hold values from 0.25 to 4
- bond_order: int32 [8192], replicated, may hold values from 0 to 8191, each once
Outputs:
- result_real: float32 [4096, 512], P('blk', 'grp')
- result_imag: float32 [4096, 512], P('blk', 'grp')
Inputs may be any that keep to these rules, and one draw needn't show every extreme that they name: bond_order names each of 0 to 8191 exactly once.
All inputs are finite; a program needn't handle non-finite values.
Results may differ from a plain program's by a relative error of at most 0.0003.
Values may be sent and summed in bfloat16 or wider, within the bound.
A program may use at most 128 MiB of HBM per device.

v0:
```python
import jax
import jax.numpy as jnp
from jax import lax
from jax.sharding import PartitionSpec as P


def taken_in(shard, axis, dim, absorb, state):
    everything = jax.tree.map(lambda a: lax.all_gather(a, axis, axis=dim, tiled=True), shard)
    return absorb(state, everything, jnp.int32(0))


def body(left_real, left_imag, right_real, right_imag, row_scale, bond_order):
    order = bond_order.astype(jnp.int32)
    perm_real = jnp.take(left_real, order, axis=1)
    perm_imag = jnp.take(left_imag, order, axis=1)

    def columns(start, count):
        return (
            lax.dynamic_slice_in_dim(perm_real, start, count, 1),
            lax.dynamic_slice_in_dim(perm_imag, start, count, 1),
        )

    empty = jnp.zeros((left_real.shape[0], right_real.shape[1]), jnp.float32)

    def add_real(carry, piece, start):
        cols_real, cols_imag = columns(start, piece.shape[0])
        return (
            carry[0] + jnp.dot(cols_real, piece, preferred_element_type=jnp.float32),
            carry[1] + jnp.dot(cols_imag, piece, preferred_element_type=jnp.float32),
        )

    def add_imag(carry, piece, start):
        cols_real, cols_imag = columns(start, piece.shape[0])
        return (
            carry[0] - jnp.dot(cols_imag, piece, preferred_element_type=jnp.float32),
            carry[1] + jnp.dot(cols_real, piece, preferred_element_type=jnp.float32),
        )

    partial_value = taken_in(right_real, "blk", 0, add_real, (empty, empty))
    raw_real, raw_imag = taken_in(right_imag, "blk", 0, add_imag, partial_value)
    scaled_real = raw_real * row_scale[:, None]
    scaled_imag = raw_imag * row_scale[:, None]
    local_total = jnp.sum(scaled_real * scaled_real + scaled_imag * scaled_imag)
    total = lax.psum(local_total, ("blk", "grp"))
    entries = (
        scaled_real.shape[0] * scaled_real.shape[1] * lax.axis_size("blk") * lax.axis_size("grp")
    )
    factor = 1.0 / jnp.sqrt(total / jnp.float32(entries))
    return (scaled_real * factor, scaled_imag * factor)


def solution(mesh):
    in_specs = (P("blk", None), P("blk", None), P("blk", "grp"), P("blk", "grp"), P("blk"), P())
    out_specs = (P("blk", "grp"), P("blk", "grp"))
    return jax.shard_map(body, mesh=mesh, in_specs=in_specs, out_specs=out_specs, check_vma=False)
```

profile of v0, /device:TPU:0, one launch (start us, length us, event | category | flops | bytes accessed | tf_op | source)
XLA Modules:
  0.0 176.5 jit_solution(7276851709117105259)
XLA Ops:
  7.2 0.0 all-gather.5.cloned.1.call-start
  7.2 0.7 all-gather.5.cloned.1.call-update
  7.9 0.0 all-gather.3.cloned.1.call-start
  7.9 0.7 all-gather.3.cloned.1.call-update
  8.6 6.4 %copy.9 = bf16[256,8192]{0,1:T(8,128)(2,1)} copy(bf16[256,8192]{1,0:T(8,128)(2,1)} %param.9) | data formatting | bytes 8388608 | tf_op args[1]
  15.0 0.0 copy-start.1
  15.0 6.4 %copy.8 = bf16[256,8192]{0,1:T(8,128)(2,1)} copy(bf16[256,8192]{1,0:T(8,128)(2,1)} %param.8) | data formatting | bytes 8388608 | tf_op args[0]
  21.4 0.0 copy-done.1
  21.4 33.6 %gather_fusion.1 = bf16[8192,256]{1,0:T(8,128)(2,1)} fusion(bf16[256,8192]{0,1:T(8,128)(2,1)} %copy.9, s32[8192]{0:T(1024)S(1)} %fusion.20), kind=kCustom, calls=%fused_computation.1.clone | custom fusion | bytes 8421376 | tf_op jit(solution)/shard_map/jit(_take)/gather | solution.py:15
  55.0 33.6 %gather_fusion = bf16[8192,256]{1,0:T(8,128)(2,1)} fusion(bf16[256,8192]{0,1:T(8,128)(2,1)} %copy.8, s32[8192]{0:T(1024)S(1)} %fusion.20), kind=kCustom, calls=%fused_computation.clone | custom fusion | bytes 8421376 | tf_op jit(solution)/shard_map/jit(_take)/gather | solution.py:14
  88.7 0.0 all-gather.5.cloned.1.call-done
  88.7 7.4 %fusion.2 = f32[256,256]{1,0:T(8,128)S(1)} fusion(bf16[8192,256]{1,0:T(8,128)(2,1)} %all-gather.5.cloned.1.call-done, bf16[8192,256]{1,0:T(8,128)(2,1)} %gather_fusion.1, pred[8192]{0:T(1024)(128)(4,1)S(1)} %compare_and_fusion), kind=kOutput, calls=%fused_computation.4 | convolution fusion | flops 1075838976 | bytes 8658944 | tf_op jit(solution)/shard_map/dot_general | solution.py:35
  96.1 0.0 copy-start.4
  96.1 19.0 %all-gather.3.cloned.1.call-done = bf16[8192,256]{1,0:T(8,128)(2,1)} async-done(((bf16[512,256]{1,0:T(8,128)(2,1)}), bf16[8192,256]{1,0:T(8,128)(2,1)}) %all-gather.3.cloned.1.call-update) | async-done | bytes 4194320 | tf_op jit(solution)/shard_map/all_gather | solution.py:8
  115.0 0.0 copy-start
  115.0 0.0 copy-start.3
  115.0 7.7 %fusion = f32[256,256]{1,0:T(8,128)S(1)} fusion(bf16[8192,256]{1,0:T(8,128)(2,1)} %all-gather.3.cloned.1.call-done, bf16[8192,256]{1,0:T(8,128)(2,1)} %gather_fusion.1, pred[8192]{0:T(1024)(128)(4,1)S(1)} %compare_and_fusion), kind=kOutput, calls=%fused_computation.2 | convolution fusion | flops 1075838976 | bytes 8658944 | tf_op jit(solution)/shard_map/dot_general | solution.py:29
  122.8 0.0 copy-done.4
  122.8 0.0 copy-done
  122.8 0.0 copy-done.3
  122.8 0.0 copy-start.2
  122.8 2.6 %fusion.11 = f32[256,256]{1,0:T(8,128)S(1)} fusion(f32[256,256]{1,0:T(8,128)S(1)} %fusion.2, bf16[8192,256]{1,0:T(8,128)(2,1)S(1)} %copy-done.3, bf16[8192,256]{1,0:T(8,128)(2,1)S(1)} %copy-done, pred[8192]{0:T(1024)(128)(4,1)S(1)} %compare_and_fusion, f32[256]{0:T(256)S(1)} %copy-done.4), kind=kOutput, calls=%fused_computation.13 | convolution fusion | flops 1075970048 | bytes 8922112 | tf_op jit(solution)/shard_map/dot_general | solution.py:28
  125.4 0.0 copy-done.2
  125.5 3.2 %add_reduce_fusion = (f32[]{:T(128)}, f32[256,256]{1,0:T(8,128)S(1)}) fusion(f32[256,256]{1,0:T(8,128)S(1)} %fusion.11, f32[256]{0:T(256)S(1)} %copy-done.4, f32[256,256]{1,0:T(8,128)S(1)} %fusion, bf16[8192,256]{1,0:T(8,128)(2,1)S(1)} %copy-done.2, bf16[8192,256]{1,0:T(8,128)(2,1)S(1)} %copy-done, pred[8192]{0:T(1024)(128)(4,1)S(1)} %compare_and_fusion), kind=kOutput, calls=%fused_computation.16 | convolution fusion | flops 1076232192 | bytes 9184260 | tf_op jit(solution)/shard_map/dot_general | solution.py:36
  128.7 39.4 %psum.7 = f32[]{:T(128)} all-reduce(f32[]{:T(128)} %get-tuple-element.3), channel_id=1, replica_groups=mesh['blk'=16,'grp'=2] {'blk','grp'}, use_global_device_ids=true, to_apply=%region_1.3 | all-reduce | flops 1 | bytes 8 | tf_op jit(solution)/shard_map/psum | solution.py:44
  168.8 0.8 broadcast_multiply_fusion
  (2 shorter events, 0.0 us)
Async XLA Ops:
  7.2 81.5 %all-gather.5.cloned.1.call-start = ((), (), s32[]{:S(2)}) async-start(), calls=%async_computation.1 | async-start | bytes 4456448 | tf_op jit(solution)/shard_map/all_gather | solution.py:8
  7.9 107.1 %all-gather.3.cloned.1.call-start = ((), (), s32[]{:S(2)}) async-start(), calls=%async_computation | async-start | bytes 4456448 | tf_op jit(solution)/shard_map/all_gather | solution.py:8
  15.0 6.4 %copy-start.1 = (s32[8192]{0:T(1024)S(1)}, s32[8192]{0:T(1024)}, u32[]{:S(2)}) copy-start(s32[8192]{0:T(1024)} %param.13) | copy-start | bytes 98308
  96.1 26.7 %copy-start.4 = (f32[256]{0:T(256)S(1)}, f32[256]{0:T(256)}, u32[]{:S(2)}) copy-start(f32[256]{0:T(256)} %param.12) | copy-start | bytes 3076
  115.0 7.8 %copy-start = (bf16[8192,256]{1,0:T(8,128)(2,1)S(1)}, bf16[8192,256]{1,0:T(8,128)(2,1)}, u32[]{:S(2)}) copy-start(bf16[8192,256]{1,0:T(8,128)(2,1)} %gather_fusion) | copy-start | bytes 12582916
  115.0 7.8 %copy-start.3 = (bf16[8192,256]{1,0:T(8,128)(2,1)S(1)}, bf16[8192,256]{1,0:T(8,128)(2,1)}, u32[]{:S(2)}) copy-start(bf16[8192,256]{1,0:T(8,128)(2,1)} %all-gather.3.cloned.1.call-done) | copy-start | bytes 12582916
  122.8 2.6 %copy-start.2 = (bf16[8192,256]{1,0:T(8,128)(2,1)S(1)}, bf16[8192,256]{1,0:T(8,128)(2,1)}, u32[]{:S(2)}) copy-start(bf16[8192,256]{1,0:T(8,128)(2,1)} %all-gather.5.cloned.1.call-done) | copy-start | bytes 12582916
Sparse Core Ops, SparseCore 0:
  10.1 53.2 all-gather.4
  65.6 49.3 all-gather.2
where the time goes:
time: 177 us; the launch traced here: 176 us
  local copies, waits for them, and re-layouts  80 us (45%)
  blocking collectives  39.4 us (22%)
  matrix products  20.9 us (12%)
  waiting for transfers between devices  20.4 us (12%)
  between operations  14.8 us (8%)
    psum x1, blocking collectives, body(): total = lax.psum(local_total, ('blk', 'grp'))  39.4 us
    gather x1, local copies, waits for them, and re-layouts, body(): perm_imag = jnp.take(left_imag, order, axis=1)  33.6 us
    gather x1, local copies, waits for them, and re-layouts, body(): perm_real = jnp.take(left_real, order, axis=1)  33.6 us
    all_gather x2, waiting for transfers between devices, taken_in(): lax.all_gather(a, axis, axis=dim, tiled=True)  19 us
    unnamed x12, local copies, waits for them, and re-layouts  12.8 us
    dot_general x1, matrix products, add_real(): jnp.dot(cols_imag, piece, preferred_element_type=jnp.float32)  7.74 us
    dot_general x1, matrix products, add_imag(): jnp.dot(cols_imag, piece, preferred_element_type=jnp.float32)  7.37 us
  transfers between devices with their start and end apart: 2, of which 1 were waited for; matrix products, arithmetic and copies ran while one was open for 50% of the time, Pallas kernels for 0%

commit v1 on v0

v1 whole, which is shorter than its diff:
```python
import functools

import jax
import jax.numpy as jnp
from jax import lax
from jax.experimental import pallas as pl
from jax.experimental.pallas import tpu as pltpu
from jax.sharding import PartitionSpec as P

MESH = pl.DeviceIdType.MESH
LANES = 128
GROUP = 256
PIECES = 4
STAGES = 8
UNROLL = 16


def kernel(
    devices,
    lr_hbm, li_hbm, rr_ref, ri_ref, scale_ref, order_ref,
    out_r, out_i, total_ref,
    left_v, table, picked, perm, held, acc,
    left_sem, ring_send, ring_recv, pair_send, pair_recv,
):
    rows, bond = lr_hbm.shape
    depth, cols = rr_ref.shape
    chips = devices // 2
    far = chips // 2
    per = GROUP // LANES
    words = 2 * per
    width = bond // STAGES
    piece = 2 * cols // PIECES

    me = lax.axis_index("blk")
    chip, core = me // 2, lax.rem(me, 2)
    other = 1 - core
    place = jnp.where(lax.rem(chip, 2) == 0, chip // 2, chips - 1 - chip // 2)

    def chip_at(p):
        p = lax.rem(p + 2 * chips, chips)
        return jnp.where(p < far, 2 * p, 2 * (chips - 1 - p) + 1)

    def block_at(p, which):
        return chip_at(p) * 2 + which

    partner = chip * 2 + other
    ahead = (block_at(place + 1, core), block_at(place - 1, core))

    def read_left(group, stage):
        return [
            pltpu.make_async_copy(
                src.at[pl.ds(group * GROUP, GROUP), pl.ds(stage * width, width)],
                left_v.at[n, stage],
                left_sem.at[n, stage],
            )
            for n, src in enumerate((lr_hbm, li_hbm))
        ]

    for stage in range(STAGES):
        for copy in read_left(0, stage):
            copy.start()

    barrier = pltpu.get_barrier_semaphore()
    for target in (ahead[0], ahead[1], partner):
        pl.semaphore_signal(barrier, inc=1, device_id={"blk": target}, device_id_type=MESH)

    for n, ref in enumerate((rr_ref, ri_ref)):
        held[me, n * cols:(n + 1) * cols, :] = (
            ref[...].astype(jnp.float32).T.astype(jnp.bfloat16)
        )
    acc[...] = jnp.zeros_like(acc)
    pl.semaphore_wait(barrier, 3)

    def chunk(block, c):
        return held.at[block, pl.ds(c * piece, piece), :]

    def plan(way):
        full = [(d, c) for d in range(1, far) for c in range(PIECES)]
        half = range(PIECES // 2) if way == 0 else range(PIECES // 2, PIECES)
        return full + [(far, c) for c in half]

    plans = (plan(0), plan(1))
    rounds = len(plans[0])

    def source(way, d):
        return place - d if way == 0 else place + d

    def ring_copy(way, slot, block):
        return pltpu.make_async_remote_copy(
            src_ref=chunk(block, plans[way][slot][1]),
            dst_ref=chunk(block, plans[way][slot][1]),
            send_sem=ring_send.at[way, slot],
            recv_sem=ring_recv.at[way, slot],
            device_id={"blk": ahead[way]},
            device_id_type=MESH,
        )

    def send_ring(way, slot):
        block = block_at(source(way, plans[way][slot][0] - 1), core)
        ring_copy(way, slot, block).start()

    def wait_ring(way, slot):
        block = block_at(source(way, plans[way][slot][0]), core)
        ring_copy(way, slot, block).wait_recv()

    def pair_copy(way, slot, which):
        d, c = (0, slot) if way == 2 else plans[way][slot]
        block = block_at(place if way == 2 else source(way, d), which)
        return pltpu.make_async_remote_copy(
            src_ref=chunk(block, c),
            dst_ref=chunk(block, c),
            send_sem=pair_send.at[way, slot],
            recv_sem=pair_recv.at[way, slot],
            device_id={"blk": partner},
            device_id_type=MESH,
        )

    slot_of = tuple({entry: slot for slot, entry in enumerate(p)} for p in plans)
    for slot in range(PIECES):
        for way in range(2):
            c = slot
            if (1, c) in slot_of[way]:
                send_ring(way, slot_of[way][(1, c)])
    for c in range(PIECES):
        pair_copy(2, c, core).start()

    def pass_on(slot):
        for way in range(2):
            wait_ring(way, slot)
            d, c = plans[way][slot]
            later = slot_of[way].get((d + 1, c))
            if later is not None:
                send_ring(way, later)
            pair_copy(way, slot, core).start()

    def turn(group, stage):
        for copy in read_left(group, stage):
            copy.wait()

        def step(t, _):
            at = pl.multiple_of(t * LANES, LANES)
            for n in range(2):
                for h in range(per):
                    tile = left_v[n, stage, h * LANES:(h + 1) * LANES, pl.ds(at, LANES)]
                    first = pl.multiple_of(stage * width + at, LANES)
                    table[pl.ds(first, LANES), n * per + h, :] = tile.astype(jnp.float32).T
            return 0

        lax.fori_loop(0, width // LANES, step, 0, unroll=2)

    def pick(block):
        base = block * depth

        def step(s, _):
            at = s * UNROLL
            got = []
            for u in range(UNROLL):
                got.append(table[order_ref[base + at + u]])
            for u in range(UNROLL):
                picked[at + u] = got[u]
            return 0

        lax.fori_loop(0, depth // UNROLL, step, 0)
        for w in range(words):
            perm[block, :, w * LANES:(w + 1) * LANES] = picked[:, w, :].astype(jnp.bfloat16)

    def multiply(block):
        acc[...] += jnp.dot(held[block], perm[block], preferred_element_type=jnp.float32)

    def multiply_chip(p):
        def step(which, _):
            multiply(block_at(p, which))
            return 0

        lax.fori_loop(0, 2, step, 0)

    def finish(group):
        low, high = pl.ds(0, cols), pl.ds(cols, cols)
        scale = scale_ref[:, group * GROUP:(group + 1) * GROUP]
        real = (acc[low, 0:GROUP] - acc[high, GROUP:2 * GROUP]) * scale
        imag = (acc[low, GROUP:2 * GROUP] + acc[high, 0:GROUP]) * scale
        squares = jnp.sum(real * real + imag * imag, axis=0, keepdims=True)
        total_ref[...] = squares if group == 0 else total_ref[...] + squares
        out_r[group * GROUP:(group + 1) * GROUP, :] = real.T
        out_i[group * GROUP:(group + 1) * GROUP, :] = imag.T

    def pick_some(first, last):
        lax.fori_loop(first, last, lambda b, _: (pick(b), 0)[1], 0)

    work = [functools.partial(turn, 0, s) for s in range(STAGES)]
    parts = 8
    edges = [devices * i // parts for i in range(parts + 1)]
    work += [functools.partial(pick_some, a, b) for a, b in zip(edges, edges[1:])]

    def pair_wait(d):
        for way in range(2):
            for slot, entry in enumerate(plans[way]):
                if entry[0] == d:
                    pair_copy(way, slot, other).wait_recv()

    def multiply_own():
        for c in range(PIECES):
            pair_copy(2, c, other).wait_recv()
        multiply_chip(place)

    def multiply_at(d):
        pair_wait(d)

        def step(i, _):
            side, which = i // 2, lax.rem(i, 2)
            multiply(block_at(place - d + 2 * d * side, which))
            return 0

        lax.fori_loop(0, 4 if d < far else 2, step, 0)

    work.append(multiply_own)
    early = max(1, rounds * 5 // 7)
    done = 0
    todo = list(range(1, far + 1))
    for slot in range(rounds):
        until = len(work) if slot >= early else len(work) * (slot + 1) // (early + 1)
        for item in work[done:until]:
            item()
        done = max(done, until)
        if done == len(work) and todo and todo[0] < plans[0][slot][0]:
            multiply_at(todo.pop(0))
        pass_on(slot)
    for d in todo:
        multiply_at(d)
    finish(0)

    for group in range(1, rows // GROUP):
        for stage in range(STAGES):
            for copy in read_left(group, stage):
                copy.start()
        for stage in range(STAGES):
            turn(group, stage)
        pick_some(0, devices)
        acc[...] = jnp.zeros_like(acc)
        lax.fori_loop(0, devices, lambda b, _: (multiply(b), 0)[1], 0)
        finish(group)

    for way in range(2):
        for slot in range(rounds):
            block = block_at(source(way, plans[way][slot][0] - 1), core)
            ring_copy(way, slot, block).wait_send()
            pair_copy(way, slot, core).wait_send()
    for c in range(PIECES):
        pair_copy(2, c, core).wait_send()


def body(devices, left_real, left_imag, right_real, right_imag, row_scale, bond_order):
    rows, bond = left_real.shape
    depth, cols = right_real.shape
    rounds = PIECES * devices // 4
    vmem = pl.BlockSpec(memory_space=pltpu.VMEM)
    far = pl.BlockSpec(memory_space=pl.ANY)
    words = 2 * GROUP // LANES
    out = jax.ShapeDtypeStruct((rows, cols), jnp.float32)
    real, imag, squares = pl.pallas_call(
        functools.partial(kernel, devices),
        out_shape=(out, out, jax.ShapeDtypeStruct((1, GROUP), jnp.float32)),
        in_specs=[far, far, vmem, vmem, vmem, pl.BlockSpec(memory_space=pltpu.SMEM)],
        out_specs=(vmem, vmem, vmem),
        scratch_shapes=[
            pltpu.VMEM((2, STAGES, GROUP, bond // STAGES), jnp.bfloat16),
            pltpu.VMEM((bond, words, LANES), jnp.float32),
            pltpu.VMEM((depth, words, LANES), jnp.float32),
            pltpu.VMEM((devices, depth, 2 * GROUP), jnp.bfloat16),
            pltpu.VMEM((devices, 2 * cols, depth), jnp.bfloat16),
            pltpu.VMEM((2 * cols, 2 * GROUP), jnp.float32),
            pltpu.SemaphoreType.DMA((2, STAGES)),
            pltpu.SemaphoreType.DMA((2, rounds)),
            pltpu.SemaphoreType.DMA((2, rounds)),
            pltpu.SemaphoreType.DMA((3, rounds)),
            pltpu.SemaphoreType.DMA((3, rounds)),
        ],
        compiler_params=pltpu.CompilerParams(
            collective_id=0, has_side_effects=True, vmem_limit_bytes=60 * 1024 * 1024
        ),
    )(left_real, left_imag, right_real, right_imag, row_scale.reshape(1, rows), bond_order)
    total = lax.psum(jnp.sum(squares), ("blk", "grp"))
    entries = rows * cols * lax.axis_size("blk") * lax.axis_size("grp")
    factor = 1.0 / jnp.sqrt(total / jnp.float32(entries))
    return real * factor, imag * factor


def solution(mesh):
    in_specs = (P("blk", None), P("blk", None), P("blk", "grp"), P("blk", "grp"), P("blk"), P())
    out_specs = (P("blk", "grp"), P("blk", "grp"))
    return jax.shard_map(
        functools.partial(body, mesh.shape["blk"]),
        mesh=mesh, in_specs=in_specs, out_specs=out_specs, check_vma=False,
    )
```

time: 177 us -> 110 us (0.62)
  local copies, waits for them, and re-layouts: 80 us -> 0 us
  Pallas kernels: 0 us -> 64.3 us
  matrix products: 20.9 us -> 0 us
  waiting for transfers between devices: 20.4 us -> 0 us
  between operations: 14.8 us -> 1.33 us
  other arithmetic: 0.85 us -> 3.15 us
    gather x2 -> x0, local copies, waits for them, and re-layouts: 67.2 us -> none  [the longest x1 33.6 us: body(): perm_imag = jnp.take(left_imag, order, axis=1)]
    pallas_call x0 -> x1, Pallas kernels: none -> 64.3 us  [body(): pl.pallas_call(functools.partial(kernel, devices), out_shape=(out, out, j...]
    dot_general x4 -> x0, matrix products: 20.9 us -> none  [the longest x1 7.74 us: add_real(): jnp.dot(cols_imag, piece, preferred_element_type=jnp.float32)]
    all_gather x2 -> x0, waiting for transfers between devices: 19 us -> none  [taken_in(): lax.all_gather(a, axis, axis=dim, tiled=True)]
    unnamed x12 -> x0, local copies, waits for them, and re-layouts: 12.8 us -> none
  transfers between devices with their start and end apart: 2 -> 0, of which waited for: 1 -> 0; matrix products, arithmetic and copies ran while one was open for 50% -> 0% of each run, Pallas kernels for 0% -> 0%
where the time goes in v1:
time: 110 us; the launch traced here: 109 us
  Pallas kernels  64.3 us (58%)
  blocking collectives  40.5 us (37%)
  other arithmetic  3.15 us (3%)
  between operations  1.33 us (1%)
    pallas_call x1, Pallas kernels, body(): pl.pallas_call(functools.partial(kernel, devices), out_shape=(out, out, j...  64.3 us
    psum x1, blocking collectives, body(): total = lax.psum(jnp.sum(squares), ('blk', 'grp'))  40.5 us

profile of v1, /device:TPU:0, one launch (start us, length us, event | category | flops | bytes accessed | tf_op | source)
XLA Modules:
  0.0 109.3 jit_solution(9251496886886528695)
XLA Ops:
  0.6 64.3 %shard_map.77 = (f32[256,256]{1,0:T(8,128)}, f32[256,256]{1,0:T(8,128)}, f32[1,256]{1,0:T(1,128)}) custom-call(bf16[256,8192]{1,0:T(8,128)(2,1)} %lr_hbm.1, bf16[256,8192]{1,0:T(8,128)(2,1)} %li_hbm.1, bf16[512,256]{1,0:T(8,128)(2,1)} %rr_ref.1, bf16[512,256]{1,0:T(8,128)(2,1)} %ri_ref.1, f32[1,256]{1,0:T(1,128)} %bitcast.1, s32[8192]{0:T(1024)} %order_ref.1), custom_call_target="tpu_custom_call" | custom-call | tf_op jit(solution)/shard_map/pallas_call | solution.py:260
  65.0 1.3 %reduce_sum.9 = f32[]{:T(128)} reduce(f32[1,256]{1,0:T(1,128)} %get-tuple-element.6, f32[]{:T(128)} %constant.2.clone.1), dimensions={0,1}, to_apply=%region_0.0 | reduce | flops 255 | bytes 1032 | tf_op jit(solution)/shard_map/reduce_sum | solution.py:282
  66.3 40.5 %psum.7 = f32[]{:T(128)} all-reduce(f32[]{:T(128)} %reduce_sum.9), channel_id=1, replica_groups=mesh['blk'=16,'grp'=2] {'blk','grp'}, use_global_device_ids=true, to_apply=%region_1.0 | all-reduce | flops 1 | bytes 8 | tf_op jit(solution)/shard_map/psum | solution.py:282
  107.5 1.9 %broadcast_multiply_fusion = (f32[256,256]{1,0:T(8,128)}, f32[256,256]{1,0:T(8,128)}) fusion(f32[256,256]{1,0:T(8,128)} %get-tuple-element.7, f32[]{:T(128)S(6)} %sqrt.3, f32[256,256]{1,0:T(8,128)} %get-tuple-element.5), kind=kLoop, calls=%fused_computation | loop fusion | flops 131072 | bytes 1048580 | tf_op jit(solution)/shard_map/mul | solution.py:285

commit v2 on v1

--- a/solution.py
+++ b/solution.py
@@ -16,11 +16,12 @@
 
 
 def kernel(
-    devices,
+    devices, groups,
     lr_hbm, li_hbm, rr_ref, ri_ref, scale_ref, order_ref,
-    out_r, out_i, total_ref,
+    out_r, out_i, factor_ref,
     left_v, table, picked, perm, held, acc,
     left_sem, ring_send, ring_recv, pair_send, pair_recv,
+    sums, group_sums, sum_send, sum_recv, group_send, group_recv,
 ):
     rows, bond = lr_hbm.shape
     depth, cols = rr_ref.shape
@@ -32,6 +33,7 @@
     piece = 2 * cols // PIECES
 
     me = lax.axis_index("blk")
+    my_group = lax.axis_index("grp")
     chip, core = me // 2, lax.rem(me, 2)
     other = 1 - core
     place = jnp.where(lax.rem(chip, 2) == 0, chip // 2, chips - 1 - chip // 2)
@@ -61,15 +63,19 @@
             copy.start()
 
     barrier = pltpu.get_barrier_semaphore()
-    for target in (ahead[0], ahead[1], partner):
+    for o in range(1, devices):
+        target = lax.rem(me + o, devices)
         pl.semaphore_signal(barrier, inc=1, device_id={"blk": target}, device_id_type=MESH)
+    for o in range(1, groups):
+        target = lax.rem(my_group + o, groups)
+        pl.semaphore_signal(barrier, inc=1, device_id={"grp": target}, device_id_type=MESH)
 
     for n, ref in enumerate((rr_ref, ri_ref)):
         held[me, n * cols:(n + 1) * cols, :] = (
             ref[...].astype(jnp.float32).T.astype(jnp.bfloat16)
         )
     acc[...] = jnp.zeros_like(acc)
-    pl.semaphore_wait(barrier, 3)
+    pl.semaphore_wait(barrier, devices + groups - 2)
 
     def chunk(block, c):
         return held.at[block, pl.ds(c * piece, piece), :]
@@ -157,12 +163,14 @@
             for u in range(UNROLL):
                 got.append(table[order_ref[base + at + u]])
             for u in range(UNROLL):
-                picked[at + u] = got[u]
+                picked[pl.ds(pl.multiple_of((at + u) * words, words), words), :] = got[u]
             return 0
 
         lax.fori_loop(0, depth // UNROLL, step, 0)
         for w in range(words):
-            perm[block, :, w * LANES:(w + 1) * LANES] = picked[:, w, :].astype(jnp.bfloat16)
+            perm[block, :, w * LANES:(w + 1) * LANES] = picked[
+                pl.ds(w, depth, stride=words), :
+            ].astype(jnp.bfloat16)
 
     def multiply(block):
         acc[...] += jnp.dot(held[block], perm[block], preferred_element_type=jnp.float32)
@@ -173,6 +181,37 @@
             return 0
 
         lax.fori_loop(0, 2, step, 0)
+
+    def sum_copy(o):
+        return pltpu.make_async_remote_copy(
+            src_ref=sums.at[me],
+            dst_ref=sums.at[me],
+            send_sem=sum_send.at[o - 1],
+            recv_sem=sum_recv.at[o - 1],
+            device_id={"blk": lax.rem(me + o, devices)},
+            device_id_type=MESH,
+        )
+
+    def sum_wait(o):
+        block = lax.rem(me + devices - o, devices)
+        pltpu.make_async_remote_copy(
+            src_ref=sums.at[block],
+            dst_ref=sums.at[block],
+            send_sem=sum_send.at[o - 1],
+            recv_sem=sum_recv.at[o - 1],
+            device_id={"blk": block},
+            device_id_type=MESH,
+        ).wait_recv()
+
+    def group_copy(o, which):
+        return pltpu.make_async_remote_copy(
+            src_ref=group_sums.at[which],
+            dst_ref=group_sums.at[which],
+            send_sem=group_send.at[o - 1],
+            recv_sem=group_recv.at[o - 1],
+            device_id={"grp": lax.rem(my_group + o, groups)},
+            device_id_type=MESH,
+        )
 
     def finish(group):
         low, high = pl.ds(0, cols), pl.ds(cols, cols)
@@ -180,8 +219,12 @@
         real = (acc[low, 0:GROUP] - acc[high, GROUP:2 * GROUP]) * scale
         imag = (acc[low, GROUP:2 * GROUP] + acc[high, 0:GROUP]) * scale
         squares = jnp.sum(real * real + imag * imag, axis=0, keepdims=True)
-        total_ref[...] = squares if group == 0 else total_ref[...] + squares
+        folded = sum(squares[:, h * LANES:(h + 1) * LANES] for h in range(per))
+        sums[me] = folded if group == 0 else sums[me] + folded
         out_r[group * GROUP:(group + 1) * GROUP, :] = real.T
+        if group == rows // GROUP - 1:
+            for o in range(1, devices):
+                sum_copy(o).start()
         out_i[group * GROUP:(group + 1) * GROUP, :] = imag.T
 
     def pick_some(first, last):
@@ -240,6 +283,9 @@
         lax.fori_loop(0, devices, lambda b, _: (multiply(b), 0)[1], 0)
         finish(group)
 
+    for o in range(1, devices):
+        sum_wait(o)
+    group_sums[my_group] = jnp.sum(sums[...], axis=0)
     for way in range(2):
         for slot in range(rounds):
             block = block_at(source(way, plans[way][slot][0] - 1), core)
@@ -247,9 +293,19 @@
             pair_copy(way, slot, core).wait_send()
     for c in range(PIECES):
         pair_copy(2, c, core).wait_send()
-
-
-def body(devices, left_real, left_imag, right_real, right_imag, row_scale, bond_order):
+    for o in range(1, devices):
+        sum_copy(o).wait_send()
+    for o in range(1, groups):
+        group_copy(o, my_group).start()
+    for o in range(1, groups):
+        group_copy(o, lax.rem(my_group + groups - o, groups)).wait_recv()
+    total = jnp.sum(jnp.sum(group_sums[...], axis=0), axis=1, keepdims=True)
+    factor_ref[...] = 1.0 / jnp.sqrt(total / jnp.float32(rows * cols * devices * groups))
+    for o in range(1, groups):
+        group_copy(o, my_group).wait_send()
+
+
+def body(devices, groups, left_real, left_imag, right_real, right_imag, row_scale, bond_order):
     rows, bond = left_real.shape
     depth, cols = right_real.shape
     rounds = PIECES * devices // 4
@@ -257,15 +313,15 @@
     far = pl.BlockSpec(memory_space=pl.ANY)
     words = 2 * GROUP // LANES
     out = jax.ShapeDtypeStruct((rows, cols), jnp.float32)
-    real, imag, squares = pl.pallas_call(
-        functools.partial(kernel, devices),
-        out_shape=(out, out, jax.ShapeDtypeStruct((1, GROUP), jnp.float32)),
+    real, imag, factor = pl.pallas_call(
+        functools.partial(kernel, devices, groups),
+        out_shape=(out, out, jax.ShapeDtypeStruct((1, 1), jnp.float32)),
         in_specs=[far, far, vmem, vmem, vmem, pl.BlockSpec(memory_space=pltpu.SMEM)],
         out_specs=(vmem, vmem, vmem),
         scratch_shapes=[
             pltpu.VMEM((2, STAGES, GROUP, bond // STAGES), jnp.bfloat16),
             pltpu.VMEM((bond, words, LANES), jnp.float32),
-            pltpu.VMEM((depth, words, LANES), jnp.float32),
+            pltpu.VMEM((depth * words, LANES), jnp.float32),
             pltpu.VMEM((devices, depth, 2 * GROUP), jnp.bfloat16),
             pltpu.VMEM((devices, 2 * cols, depth), jnp.bfloat16),
             pltpu.VMEM((2 * cols, 2 * GROUP), jnp.float32),
@@ -274,14 +330,17 @@
             pltpu.SemaphoreType.DMA((2, rounds)),
             pltpu.SemaphoreType.DMA((3, rounds)),
             pltpu.SemaphoreType.DMA((3, rounds)),
+            pltpu.VMEM((devices, 1, LANES), jnp.float32),
+            pltpu.VMEM((groups, 1, LANES), jnp.float32),
+            pltpu.SemaphoreType.DMA((devices - 1,)),
+            pltpu.SemaphoreType.DMA((devices - 1,)),
+            pltpu.SemaphoreType.DMA((groups - 1,)),
+            pltpu.SemaphoreType.DMA((groups - 1,)),
         ],
         compiler_params=pltpu.CompilerParams(
             collective_id=0, has_side_effects=True, vmem_limit_bytes=60 * 1024 * 1024
         ),
     )(left_real, left_imag, right_real, right_imag, row_scale.reshape(1, rows), bond_order)
-    total = lax.psum(jnp.sum(squares), ("blk", "grp"))
-    entries = rows * cols * lax.axis_size("blk") * lax.axis_size("grp")
-    factor = 1.0 / jnp.sqrt(total / jnp.float32(entries))
     return real * factor, imag * factor
 
 
@@ -289,6 +348,6 @@
     in_specs = (P("blk", None), P("blk", None), P("blk", "grp"), P("blk", "grp"), P("blk"), P())
     out_specs = (P("blk", "grp"), P("blk", "grp"))
     return jax.shard_map(
-        functools.partial(body, mesh.shape["blk"]),
+        functools.partial(body, mesh.shape["blk"], mesh.shape["grp"]),
         mesh=mesh, in_specs=in_specs, out_specs=out_specs, check_vma=False,
     )

time: 110 us -> 63.7 us (0.58)
  blocking collectives: 40.5 us -> 0 us
  Pallas kernels: 64.3 us -> 60.4 us
    psum x1 -> x0, blocking collectives: 40.5 us -> none  [body(): total = lax.psum(jnp.sum(squares), ('blk', 'grp'))]
    pallas_call x1, Pallas kernels: 64.3 us -> 60.4 us  [body(): pl.pallas_call(functools.partial(kernel, devices, groups), out_shape=(out...]
    reduce_sum x1 -> x0, other arithmetic: 1.29 us -> none  [body(): total = lax.psum(jnp.sum(squares), ('blk', 'grp'))]
where the time goes in v2:
time: 63.7 us; the launch traced here: 63.5 us
  Pallas kernels  60.4 us (95%)
  other arithmetic  2.49 us (4%)
  between operations  0.64 us (1%)
    pallas_call x1, Pallas kernels, body(): pl.pallas_call(functools.partial(kernel, devices, groups), out_shape=(out...  60.4 us
    mul x1, other arithmetic, body(): return (real * factor, imag * factor)  2.49 us

profile of v2, /device:TPU:0, one launch (start us, length us, event | category | flops | bytes accessed | tf_op | source)
XLA Modules:
  0.0 63.5 jit_solution(16354811033390775650)
XLA Ops:
  0.6 60.4 %shard_map.77 = (f32[256,256]{1,0:T(8,128)}, f32[256,256]{1,0:T(8,128)}, f32[1,1]{1,0:T(1,128)}) custom-call(bf16[256,8192]{1,0:T(8,128)(2,1)} %lr_hbm.1, bf16[256,8192]{1,0:T(8,128)(2,1)} %li_hbm.1, bf16[512,256]{1,0:T(8,128)(2,1)} %rr_ref.1, bf16[512,256]{1,0:T(8,128)(2,1)} %ri_ref.1, f32[1,256]{1,0:T(1,128)} %bitcast.2, s32[8192]{0:T(1024)} %order_ref.1), custom_call_target="tpu_custom_call" | custom-call | tf_op jit(solution)/shard_map/pallas_call | solution.py:316
  61.0 2.5 %broadcast_multiply_fusion = (f32[256,256]{1,0:T(8,128)}, f32[256,256]{1,0:T(8,128)}) fusion(f32[256,256]{1,0:T(8,128)} %get-tuple-element.7, f32[]{:T(128)} %bitcast.1, f32[256,256]{1,0:T(8,128)} %get-tuple-element.5), kind=kLoop, calls=%fused_computation | loop fusion | flops 131072 | bytes 1048580 | tf_op jit(solution)/shard_map/mul | solution.py:344
